TPU v7x, 32 devices: a whole 2x2x4 slice. The times are simulated.
32 devices in a mesh: band: 16 (over z, y, core), spin: 2 (over x).
Axes of the slice: x: 2, y: 2, z: 4, core: 2. Of those that a mesh axis runs over, the one named last changes fastest.
Arguments:
- coefficients: bfloat16 [2, 2, 32, 524288], P('spin', None, 'band'), may hold values from -1 to 1
- occupation: int32 [2, 32], P('spin', 'band'), may hold values from 0 to 1000
- miller: int32 [3, 524288], P(None, ('band', 'spin')), may hold values from -8 to 8
- density: float32 [2, 256, 128, 128], P('spin', 'band'), may hold values from 0.25 to 2
- local_factor: float32 [2, 256, 128, 128], P(None, None, 'band'), may hold values from -1.2 to 1.2
Outputs:
- stress: float32 [6], replicated
- kinetic_density: float32 [524288], P(('band', 'spin'))
- gradient_square: float32 [2, 256, 128, 128], P('spin', 'band')
All inputs are finite; a program needn't handle non-finite values.
Results may differ from a plain program's by a relative error of at most 0.0003.
Values sent between devices are 32-bit elements; how exact they have to be, the bound alone decides.
No kernel may reach another device: no remote copies, remote signals or barrier semaphores. Data moves between devices by JAX's collectives and lax.ppermute only.
A program may use at most 64 MiB of HBM per device.

v0:
```python
import jax
import jax.numpy as jnp
from jax import lax
from jax.sharding import PartitionSpec as P

NPW = 524288
NX = 128
NY = 128
NZ = 256
occupation_unit = 1000.0
kpoint = (0.25, 0.125, 0.375)
spacing = 0.25


def derivative_table(length):
    row_index = jnp.arange(length, dtype=jnp.int32)[:, None]
    col_index = jnp.arange(length, dtype=jnp.int32)[None, :]
    wrapped = jnp.mod(row_index - col_index, length)
    angles = jnp.pi / length * wrapped.astype(jnp.float32)
    on_diagonal = wrapped == 0
    sines = jnp.where(on_diagonal, 1.0, jnp.sin(angles))
    parity = 1.0 - 2.0 * jnp.mod(wrapped, 2).astype(jnp.float32)
    return jnp.where(on_diagonal, 0.0, 0.5 * parity * jnp.cos(angles) / sines)


def fourier_tables(length):
    positions = jnp.arange(length, dtype=jnp.int32)
    phases = jnp.mod(positions[:, None] * positions[None, :], length).astype(jnp.float32) * (
        2.0 * jnp.pi / length
    )
    return (jnp.cos(phases), jnp.sin(phases))


def frequencies(length):
    positions = jnp.arange(length, dtype=jnp.int32)
    signed = jnp.where(positions >= length // 2, positions - length, positions)
    return 2.0 * jnp.pi / length * signed.astype(jnp.float32)


def six_sums(weighting, first_axis, second_axis, third_axis):
    return jnp.stack(
        [
            jnp.sum(weighting * first_axis * first_axis),
            jnp.sum(weighting * second_axis * second_axis),
            jnp.sum(weighting * third_axis * third_axis),
            jnp.sum(weighting * second_axis * third_axis),
            jnp.sum(weighting * first_axis * third_axis),
            jnp.sum(weighting * first_axis * second_axis),
        ]
    )


def xc_terms(dens_part, grad_x, grad_y, grad_z, cell_count):
    square = grad_x * grad_x + grad_y * grad_y + grad_z * grad_z
    kernel = dens_part ** (-1.0 / 3.0) / (1.0 + square / (4.0 * dens_part * dens_part + 1.0))
    return (square, -six_sums(kernel, grad_x, grad_y, grad_z) / cell_count)


def shards(coefficients, occupation, miller, density, local_factor):
    highest = lax.Precision.HIGHEST
    weights = occupation.astype(jnp.float32) / occupation_unit
    piece = coefficients.astype(jnp.float32)
    squares = piece[0, 0] * piece[0, 0] + piece[0, 1] * piece[0, 1]
    kinetic_weight = lax.psum_scatter(
        jnp.dot(weights[0], squares, precision=highest),
        ("band", "spin"),
        scatter_dimension=0,
        tiled=True,
    )
    kvec = jnp.array(kpoint, jnp.float32)
    gvec = spacing * (miller.astype(jnp.float32) + kvec[:, None])
    kinetic_density = 0.5 * (gvec[0] ** 2 + gvec[1] ** 2 + gvec[2] ** 2) * kinetic_weight
    kinetic_stress = -six_sums(kinetic_weight, gvec[0], gvec[1], gvec[2]) / NPW
    band_devices = lax.axis_size("band")
    cell_count = density.shape[1] * band_devices * density.shape[2] * density.shape[3]
    deriv_x = derivative_table(NX)
    deriv_y = derivative_table(NY)
    deriv_z = derivative_table(NZ)
    cosine_x, sine_x = fourier_tables(NX)
    cosine_y, sine_y = fourier_tables(NY)
    cosine_z, sine_z = fourier_tables(NZ)
    grad_x = jnp.einsum("ik,szky->sziy", deriv_x, density, precision=highest)
    grad_y = jnp.einsum("ik,szxk->szxi", deriv_y, density, precision=highest)
    along_real = jnp.einsum("mj,szxj->szxm", cosine_y, density, precision=highest)
    along_imag = -jnp.einsum("mj,szxj->szxm", sine_y, density, precision=highest)
    plane_real = jnp.einsum("mj,szjy->szmy", cosine_x, along_real, precision=highest) + jnp.einsum(
        "mj,szjy->szmy", sine_x, along_imag, precision=highest
    )
    plane_imag = jnp.einsum("mj,szjy->szmy", cosine_x, along_imag, precision=highest) - jnp.einsum(
        "mj,szjy->szmy", sine_x, along_real, precision=highest
    )
    dens_col, real_col, imag_col = (
        lax.all_to_all(density, "band", split_axis=2, concat_axis=1, tiled=True),
        lax.all_to_all(plane_real, "band", split_axis=2, concat_axis=1, tiled=True),
        lax.all_to_all(plane_imag, "band", split_axis=2, concat_axis=1, tiled=True),
    )
    gradz_col = jnp.einsum("ik,skxy->sixy", deriv_z, dens_col, precision=highest)
    grad_z = lax.all_to_all(gradz_col, "band", split_axis=1, concat_axis=2, tiled=True)
    gradient_square, xc_stress = xc_terms(density, grad_x, grad_y, grad_z, cell_count)
    spec_real = (
        jnp.einsum("mj,jxy->mxy", cosine_z, real_col[0], precision=highest)
        + jnp.einsum("mj,jxy->mxy", sine_z, imag_col[0], precision=highest)
    ) / cell_count
    spec_imag = (
        jnp.einsum("mj,jxy->mxy", cosine_z, imag_col[0], precision=highest)
        - jnp.einsum("mj,jxy->mxy", sine_z, real_col[0], precision=highest)
    ) / cell_count
    total_real, total_imag = lax.psum((spec_real, spec_imag), "spin")
    local_rows = real_col.shape[2]
    first_column = lax.axis_index("band") * local_rows
    freq_z = frequencies(NZ)[:, None, None]
    freq_x = lax.dynamic_slice_in_dim(frequencies(NX), first_column, local_rows, 0)[None, :, None]
    freq_y = frequencies(NY)[None, None, :]
    length_sq = freq_x * freq_x + freq_y * freq_y + freq_z * freq_z
    positive = length_sq > 0
    inverse = jnp.where(positive, 1.0 / jnp.where(positive, length_sq, 1.0), 0.0)
    hartree_weight = 4.0 * jnp.pi * (total_real * total_real + total_imag * total_imag) * inverse
    diagonal = jnp.array([1.0, 1.0, 1.0, 0.0, 0.0, 0.0], jnp.float32)
    hartree_stress = 2.0 * six_sums(
        hartree_weight * inverse, freq_x, freq_y, freq_z
    ) - diagonal * jnp.sum(hartree_weight)
    local_weight = 2.0 * (total_real * local_factor[0] + total_imag * local_factor[1])
    local_stress = six_sums(local_weight, freq_x, freq_y, freq_z)
    spin_share = 1.0 / lax.axis_size("spin")
    partial_stress = kinetic_stress + spin_share * (hartree_stress + local_stress) + xc_stress
    stress = lax.psum(partial_stress, ("band", "spin"))
    return (stress, kinetic_density, gradient_square)


def solution(mesh):
    return jax.shard_map(
        shards,
        mesh=mesh,
        in_specs=(
            P("spin", None, "band", None),
            P("spin", "band"),
            P(None, ("band", "spin")),
            P("spin", "band", None, None),
            P(None, None, "band", None),
        ),
        out_specs=(P(), P(("band", "spin")), P("spin", "band", None, None)),
        check_vma=False,
    )
```

profile of v0, /device:TPU:0, one launch (start us, length us, event | category | flops | bytes accessed | tf_op | source)
XLA Modules:
  0.0 325.3 jit_solution(17758232457839028548)
XLA Ops:
  7.2 2.5 fusion.6
  9.7 2.5 convolution_bitcast_fusion.2
  12.2 1.2 fusion.99
  13.4 1.2 fusion.4
  14.6 1.4 copy.29
  16.1 7.5 %all-to-all-start.1 = ((f32[1,16,128,128]{3,1,0,2:T(8,128)}), f32[1,16,128,128]{3,1,0,2:T(8,128)}, u32[]{:S(2)}, u32[]{:S(2)}) async-start(f32[1,16,128,128]{3,1,0,2:T(8,128)} %copy.29), calls=%async_computation.1 | async-start | bytes 2097152 | tf_op jit(solution)/shard_map/all_to_all | solution.py:95
  23.5 0.0 copy-start.5
  23.5 0.4 all-reduce.5.cloned.1.call-start
  24.0 4.7 %convert_element_type.102 = f32[1,2,2,524288]{3,2,1,0:T(2,128)S(1)} convert(bf16[1,2,2,524288]{3,2,1,0:T(2,128)(2,1)} %param.7) | non-fusion elementwise | flops 2097152 | bytes 12582912 | tf_op jit(solution)/shard_map/convert_element_type | solution.py:62
  28.7 0.0 copy-done.5
  28.7 0.0 copy-start
  28.7 17.0 %fusion.2 = f32[1,524288]{1,0:T(1,128)} fusion(f32[1,2,2,524288]{3,2,1,0:T(2,128)S(1)} %convert_element_type.102, s32[1,2]{1,0:T(1,128)S(1)} %copy-done.5), kind=kOutput, calls=%fused_computation.4 | convolution fusion | flops 15728644 | bytes 10485768 | tf_op jit(solution)/shard_map/dot_general | solution.py:65
  45.8 0.0 all-reduce.5.cloned.1.call-update
  45.8 0.0 copy-done
  45.8 1.6 copy.35
  47.4 1.2 fusion.101
  48.6 0.0 copy-start.2
  48.6 0.0 copy-start.3
  48.6 1.2 fusion.5
  49.9 1.4 copy.26
  51.3 0.1 fusion.201
  51.4 0.0 all-to-all-done.1
  51.4 6.0 %all-to-all-start = ((f32[1,16,128,128]{3,1,0,2:T(8,128)}), f32[1,16,128,128]{3,1,0,2:T(8,128)S(1)}, u32[]{:S(2)}, u32[]{:S(2)}) async-start(f32[1,16,128,128]{3,1,0,2:T(8,128)} %copy.26), calls=%async_computation | async-start | bytes 2097152 | tf_op jit(solution)/shard_map/all_to_all | solution.py:94
  57.3 0.0 copy-done.2
  57.4 0.0 copy-done.3
  57.4 0.1 add_multiply_fusion
  57.5 29.4 %all-to-all-done = f32[1,16,128,128]{3,1,0,2:T(8,128)S(1)} async-done(((f32[1,16,128,128]{3,1,0,2:T(8,128)}), f32[1,16,128,128]{3,1,0,2:T(8,128)S(1)}, u32[]{:S(2)}, u32[]{:S(2)}) %all-to-all-start) | async-done | bytes 1048608 | tf_op jit(solution)/shard_map/all_to_all | solution.py:94
  86.8 19.7 %all-to-all-start.2 = ((f32[1,16,128,128]{3,1,0,2:T(8,128)}), f32[1,16,128,128]{3,1,0,2:T(8,128)}, u32[]{:S(2)}, u32[]{:S(2)}) async-start(f32[1,16,128,128]{3,1,0,2:T(8,128)} %copy.35), calls=%async_computation.2 | async-start | bytes 2097152 | tf_op jit(solution)/shard_map/all_to_all | solution.py:93
  106.5 0.1 fusion.204
  106.7 1.6 copy.59
  108.2 0.6 copy.31
  108.8 0.3 copy.60
  109.2 0.6 copy.28
  109.8 20.6 %all-to-all-done.2 = f32[1,16,128,128]{3,1,0,2:T(8,128)} async-done(((f32[1,16,128,128]{3,1,0,2:T(8,128)}), f32[1,16,128,128]{3,1,0,2:T(8,128)}, u32[]{:S(2)}, u32[]{:S(2)}) %all-to-all-start.2) | async-done | bytes 1048608 | tf_op jit(solution)/shard_map/all_to_all | solution.py:93
  130.4 1.3 copy.36
  131.7 2.2 convolution_bitcast_fusion
  134.0 1.6 copy.37
  135.6 6.9 %all-to-all-start.3 = ((f32[1,256,8,128]{3,2,0,1:T(8,128)}), f32[1,256,8,128]{3,2,0,1:T(8,128)}, u32[]{:S(2)}, u32[]{:S(2)}) async-start(f32[1,256,8,128]{3,2,0,1:T(8,128)} %copy.37), calls=%async_computation.3 | async-start | bytes 2097152 | tf_op jit(solution)/shard_map/all_to_all | solution.py:98
  142.4 0.0 all-reduce.7.cloned.1.call-start
  142.5 2.0 fusion.45
  144.5 2.0 fusion.47
  146.5 3.1 fusion.7
  149.6 3.0 fusion.8
  152.6 0.0 all-reduce.7.cloned.1.call-update
  152.7 2.3 convolution_bitcast_fusion.1
  155.0 0.1 broadcast_add_fusion
  155.1 1.7 fusion.203
  156.8 44.9 %all-reduce.5.cloned.1.call-done = f32[524288]{0:T(1024)} async-done(((f32[524288]{0:T(1024)}), f32[524288]{0:T(1024)}) %all-reduce.5.cloned.1.call-update) | async-done | bytes 2097168
  201.7 2.2 multiply_reduce_fusion.13
  203.9 3.7 %stack.90 = f32[6]{0:T(128)S(1)} concatenate(f32[1]{0:T(128)} %bitcast.5, f32[1]{0:T(128)} %bitcast.7, f32[1]{0:T(128)} %bitcast.9, f32[1]{0:T(128)} %bitcast.10, f32[1]{0:T(128)} %bitcast.11, f32[1]{0:T(128)} %bitcast.12), dimensions={0} | concatenate | bytes 48 | tf_op jit(solution)/shard_map/stack | solution.py:41
  207.6 0.0 all-to-all-done.3
  207.7 0.0 copy-start.1
  207.7 5.9 %fusion.14 = (f32[1,16,128,128]{3,2,1,0:T(8,128)S(1)}, f32[1,16,128,128]{3,2,1,0:T(8,128)}, f32[128,16,128]{0,2,1:T(8,128)S(1)}) fusion(f32[1,16,128,128]{3,2,1,0:T(8,128)S(1)} %copy-done, f32[1,16,16,8,128]{4,3,2,1,0:T(8,128)} %bitcast.57, f32[1,16,128,128]{3,2,1,0:T(8,128)} %convolution_bitcast_fusion.1), kind=kOutput, calls=%fused_computation.27 | convolution fusion | flops 406093824 | bytes 6291456 | tf_op jit(solution)/shard_map/ik,szxk->szxi/dot_general | solution.py:83
  213.5 0.0 copy-done.1
  213.5 2.4 fusion.20
  216.0 3.8 %stack.111 = f32[6]{0:T(128)S(1)} concatenate(f32[1]{0:T(128)} %bitcast.60, f32[1]{0:T(128)} %bitcast.62, f32[1]{0:T(128)} %bitcast.64, f32[1]{0:T(128)} %bitcast.65, f32[1]{0:T(128)} %bitcast.66, f32[1]{0:T(128)} %bitcast.68), dimensions={0} | concatenate | bytes 48 | tf_op jit(solution)/shard_map/stack | solution.py:41
  219.8 46.0 %all-reduce.7.cloned.1.call-done = (f32[256,8,128]{2,0,1:T(8,128)}, f32[256,8,128]{2,0,1:T(8,128)}) async-done(((f32[256,8,128]{2,0,1:T(8,128)}, f32[256,8,128]{2,0,1:T(8,128)}), (f32[256,8,128]{2,0,1:T(8,128)}, f32[256,8,128]{2,0,1:T(8,128)})) %all-reduce.7.cloned.1.call-update) | async-done | bytes 2097168 | tf_op jit(solution)/shard_map/psum | solution.py:108
  265.9 2.8 fusion.121
  268.7 1.9 multiply_reduce_fusion.2
  270.6 3.8 %stack.97 = f32[6]{0:T(128)S(1)} concatenate(f32[1]{0:T(128)} %bitcast.30, f32[1]{0:T(128)} %bitcast.31, f32[1]{0:T(128)} %bitcast.32, f32[1]{0:T(128)} %bitcast.33, f32[1]{0:T(128)} %bitcast.34, f32[1]{0:T(128)} %bitcast.35), dimensions={0} | concatenate | bytes 48 | tf_op jit(solution)/shard_map/stack | solution.py:41
  274.4 3.8 %stack.104 = f32[6]{0:T(128)S(1)} concatenate(f32[1]{0:T(128)} %bitcast.38, f32[1]{0:T(128)} %bitcast.39, f32[1]{0:T(128)} %bitcast.40, f32[1]{0:T(128)} %bitcast.41, f32[1]{0:T(128)} %bitcast.42, f32[1]{0:T(128)} %bitcast.43), dimensions={0} | concatenate | bytes 48 | tf_op jit(solution)/shard_map/stack | solution.py:41
  278.2 0.0 copy-done.4
  278.2 0.7 multiply_add_fusion
  278.9 39.3 %psum.23 = f32[6]{0:T(128)} all-reduce(f32[6]{0:T(128)S(1)} %multiply_add_fusion), channel_id=1, replica_groups=mesh['band'=16,'spin'=2] {'band','spin'}, use_global_device_ids=true, to_apply=%region_28.29 | all-reduce | flops 6 | bytes 48 | tf_op jit(solution)/shard_map/psum | solution.py:126
  (6 shorter events, 0.0 us)
Async XLA Ops:
  16.1 35.3 %all-to-all-start.1 = ((f32[1,16,128,128]{3,1,0,2:T(8,128)}), f32[1,16,128,128]{3,1,0,2:T(8,128)}, u32[]{:S(2)}, u32[]{:S(2)}) async-start(f32[1,16,128,128]{3,1,0,2:T(8,128)} %copy.29), calls=%async_computation.1 | async-start | bytes 2097152 | tf_op jit(solution)/shard_map/all_to_all | solution.py:95
  23.5 5.2 %copy-start.5 = (s32[1,2]{1,0:T(1,128)S(1)}, s32[1,2]{1,0:T(1,128)}, u32[]{:S(2)}) copy-start(s32[1,2]{1,0:T(1,128)} %param.8) | copy-start | bytes 28
  23.5 178.2 %all-reduce.5.cloned.1.call-start = ((), (), s32[]{:S(2)}) async-start(), calls=%async_computation.4 | async-start | bytes 4194304
  28.7 17.1 %copy-start = (f32[1,16,128,128]{3,2,1,0:T(8,128)S(1)}, f32[1,16,128,128]{3,2,1,0:T(8,128)}, u32[]{:S(2)}) copy-start(f32[1,16,128,128]{3,2,1,0:T(8,128)} %param.10) | copy-start | bytes 3145732
  48.6 8.7 %copy-start.2 = (s32[3,16384]{1,0:T(4,128)S(1)}, s32[3,16384]{1,0:T(4,128)}, u32[]{:S(2)}) copy-start(s32[3,16384]{1,0:T(4,128)} %param.9) | copy-start | bytes 589828
  48.6 8.7 %copy-start.3 = (f32[3]{0:T(128)S(1)}, f32[3]{0:T(128)}, u32[]{:S(2)}) copy-start(f32[3]{0:T(128)} %constant.139.clone) | copy-start | bytes 40
  51.4 35.5 %all-to-all-start = ((f32[1,16,128,128]{3,1,0,2:T(8,128)}), f32[1,16,128,128]{3,1,0,2:T(8,128)S(1)}, u32[]{:S(2)}, u32[]{:S(2)}) async-start(f32[1,16,128,128]{3,1,0,2:T(8,128)} %copy.26), calls=%async_computation | async-start | bytes 2097152 | tf_op jit(solution)/shard_map/all_to_all | solution.py:94
  86.8 43.6 %all-to-all-start.2 = ((f32[1,16,128,128]{3,1,0,2:T(8,128)}), f32[1,16,128,128]{3,1,0,2:T(8,128)}, u32[]{:S(2)}, u32[]{:S(2)}) async-start(f32[1,16,128,128]{3,1,0,2:T(8,128)} %copy.35), calls=%async_computation.2 | async-start | bytes 2097152 | tf_op jit(solution)/shard_map/all_to_all | solution.py:93
  135.6 72.1 %all-to-all-start.3 = ((f32[1,256,8,128]{3,2,0,1:T(8,128)}), f32[1,256,8,128]{3,2,0,1:T(8,128)}, u32[]{:S(2)}, u32[]{:S(2)}) async-start(f32[1,256,8,128]{3,2,0,1:T(8,128)} %copy.37), calls=%async_computation.3 | async-start | bytes 2097152 | tf_op jit(solution)/shard_map/all_to_all | solution.py:98
  142.4 123.4 %all-reduce.7.cloned.1.call-start = ((), (), s32[]{:S(2)}) async-start(), calls=%async_computation.5 | async-start | bytes 4194304 | tf_op jit(solution)/shard_map/psum | solution.py:108
  207.7 5.9 %copy-start.1 = (f32[1,16,128,128]{3,2,1,0:T(8,128)S(1)}, f32[1,16,128,128]{3,2,1,0:T(8,128)}, u32[]{:S(2)}) copy-start(f32[1,16,128,128]{3,2,1,0:T(8,128)} %convolution_bitcast_fusion.1) | copy-start | bytes 3145732
  265.8 12.4 %copy-start.4 = (f32[6]{0:T(128)S(1)}, f32[6]{0:T(128)}, u32[]{:S(2)}) copy-start(f32[6]{0:T(128)} %constant.140.clone) | copy-start | bytes 76
Sparse Core Ops, SparseCore 0:
  45.9 155.7 all-reduce.4
  204.1 61.7 all-reduce.6
where the time goes:
time: 331 us; the launch traced here: 325 us
  waiting for transfers between devices  141 us (43%)
  matrix products  47.5 us (14%)
  starting transfers between devices  40.4 us (12%)
  blocking collectives  39.3 us (12%)
  local copies, waits for them, and re-layouts  27.5 us (8%)
  other arithmetic  15.1 us (5%)
  between operations  14.5 us (4%)
    psum x1, waiting for transfers between devices, shards(): total_real, total_imag = lax.psum((spec_real, spec_imag), 'spin')  46 us
    unnamed x3, waiting for transfers between devices  45 us
    psum x1, blocking collectives, shards(): stress = lax.psum(partial_stress, ('band', 'spin'))  39.3 us
    all_to_all x1, waiting for transfers between devices, shards(): lax.all_to_all(plane_real, 'band', split_axis=2, concat_axis=1, tiled=True)  29.4 us
    all_to_all x1, waiting for transfers between devices, shards(): lax.all_to_all(density, 'band', split_axis=2, concat_axis=1, tiled=True)  20.6 us
    all_to_all x1, starting transfers between devices, shards(): lax.all_to_all(density, 'band', split_axis=2, concat_axis=1, tiled=True)  19.7 us
    dot_general x1, matrix products, shards(): jnp.dot(weights[0], squares, precision=highest)  17 us
    another operation x4, local copies, waits for them, and re-layouts, six_sums(): jnp.stack([jnp.sum(weighting * first_axis * first_axis), jnp.sum(weightin...  15.2 us
  transfers between devices with their start and end apart: 6, of which 4 were waited for; matrix products, arithmetic and copies ran while one was open for 21% of the time, Pallas kernels for 0%

commit v1 on v0

--- a/solution.py
+++ b/solution.py
@@ -10,6 +10,12 @@
 occupation_unit = 1000.0
 kpoint = (0.25, 0.125, 0.375)
 spacing = 0.25
+
+
+def trade_parts(x, axis, split, join):
+    pieces = jnp.split(x, lax.axis_size(axis), axis=split)
+    arrived = lax.all_to_all(jnp.stack(pieces), axis, 0, 0)
+    return jnp.concatenate(arrived, axis=join)
 
 
 def derivative_table(length):
@@ -91,7 +97,7 @@
     )
     dens_col, real_col, imag_col = (
         lax.all_to_all(density, "band", split_axis=2, concat_axis=1, tiled=True),
-        lax.all_to_all(plane_real, "band", split_axis=2, concat_axis=1, tiled=True),
+        trade_parts(plane_real, "band", 2, 1),
         lax.all_to_all(plane_imag, "band", split_axis=2, concat_axis=1, tiled=True),
     )
     gradz_col = jnp.einsum("ik,skxy->sixy", deriv_z, dens_col, precision=highest)

time: 331 us -> 330 us (level)
  waiting for transfers between devices: 141 us -> 133 us
  local copies, waits for them, and re-layouts: 27.5 us -> 35 us
    all_to_all x1, starting transfers between devices: 19.7 us -> 5.96 us  [shards(): lax.all_to_all(density, 'band', split_axis=2, concat_axis=1, tiled=True)]
    all_to_all x1, starting transfers between devices: 5.96 us -> 18.3 us  [trade_parts(): arrived = lax.all_to_all(jnp.stack(pieces), axis, 0, 0)]
    all_to_all x1, waiting for transfers between devices: 29.4 us -> 17.1 us  [trade_parts(): arrived = lax.all_to_all(jnp.stack(pieces), axis, 0, 0)]
    unnamed x13 -> x32, local copies, waits for them, and re-layouts: 1.61 us -> 12 us
    all_to_all x1, waiting for transfers between devices: 20.6 us -> 26.3 us  [shards(): lax.all_to_all(density, 'band', split_axis=2, concat_axis=1, tiled=True)]
  transfers between devices with their start and end apart: 6 -> 6, of which waited for: 4 -> 4; matrix products, arithmetic and copies ran while one was open for 21% -> 23% of each run, Pallas kernels for 0% -> 0%
where the time goes in v1:
time: 330 us; the launch traced here: 324 us
  waiting for transfers between devices  133 us (40%)
  matrix products  47.7 us (14%)
  starting transfers between devices  39.4 us (12%)
  blocking collectives  39.3 us (12%)
  local copies, waits for them, and re-layouts  35 us (11%)
  other arithmetic  15.1 us (5%)
  between operations  14.5 us (4%)
    psum x1, waiting for transfers between devices, shards(): total_real, total_imag = lax.psum((spec_real, spec_imag), 'spin')  46 us
    unnamed x3, waiting for transfers between devices  43.7 us
    psum x1, blocking collectives, shards(): stress = lax.psum(partial_stress, ('band', 'spin'))  39.3 us
    all_to_all x1, waiting for transfers between devices, shards(): lax.all_to_all(density, 'band', split_axis=2, concat_axis=1, tiled=True)  26.3 us
    all_to_all x1, starting transfers between devices, trade_parts(): arrived = lax.all_to_all(jnp.stack(pieces), axis, 0, 0)  18.3 us
    all_to_all x1, waiting for transfers between devices, trade_parts(): arrived = lax.all_to_all(jnp.stack(pieces), axis, 0, 0)  17.1 us
    dot_general x1, matrix products, shards(): jnp.dot(weights[0], squares, precision=highest)  17 us
    another operation x4, local copies, waits for them, and re-layouts, six_sums(): jnp.stack([jnp.sum(weighting * first_axis * first_axis), jnp.sum(weightin...  15.2 us
  transfers between devices with their start and end apart: 6, of which 4 were waited for; matrix products, arithmetic and copies ran while one was open for 23% of the time, Pallas kernels for 0%

profile of v1, /device:TPU:0, one launch (start us, length us, event | category | flops | bytes accessed | tf_op | source)
XLA Modules:
  0.0 324.1 jit_solution(8679854039511306622)
XLA Ops:
  7.2 2.5 convolution_bitcast_fusion.2
  9.7 2.5 fusion.6
  12.2 1.2 fusion.117
  13.4 1.2 fusion.4
  14.6 1.4 copy.34
  16.1 7.5 %all-to-all-start.1 = ((f32[1,16,128,128]{3,1,0,2:T(8,128)}), f32[1,16,128,128]{3,1,0,2:T(8,128)}, u32[]{:S(2)}, u32[]{:S(2)}) async-start(f32[1,16,128,128]{3,1,0,2:T(8,128)} %copy.34), calls=%async_computation.1 | async-start | bytes 2097152 | tf_op jit(solution)/shard_map/all_to_all | solution.py:101
  23.5 0.4 all-reduce.5.cloned.1.call-start
  24.0 4.7 %convert_element_type.102 = f32[1,2,2,524288]{3,2,1,0:T(2,128)S(1)} convert(bf16[1,2,2,524288]{3,2,1,0:T(2,128)(2,1)} %param.7) | non-fusion elementwise | flops 2097152 | bytes 12582912 | tf_op jit(solution)/shard_map/convert_element_type | solution.py:68
  28.7 17.0 %fusion.2 = f32[1,524288]{1,0:T(1,128)} fusion(f32[1,2,2,524288]{3,2,1,0:T(2,128)S(1)} %convert_element_type.102, s32[1,2]{1,0:T(1,128)S(1)} %copy-done.7), kind=kOutput, calls=%fused_computation.4 | convolution fusion | flops 15728644 | bytes 10485768 | tf_op jit(solution)/shard_map/dot_general | solution.py:71
  45.8 0.0 all-reduce.5.cloned.1.call-update
  45.8 1.3 fusion.119
  47.1 1.6 copy.41
  48.7 1.3 fusion.5
  50.0 0.6 fusion.111
  50.6 0.6 fusion.110
  51.2 0.6 fusion.109
  51.9 0.6 fusion.108
  52.5 0.6 fusion.107
  53.1 0.6 fusion.106
  53.7 0.6 fusion.105
  54.4 0.6 fusion.104
  55.0 0.6 fusion.103
  55.6 0.6 fusion.102
  56.2 0.6 fusion.101
  56.9 0.6 fusion.100
  57.5 0.6 fusion.99
  58.1 0.6 fusion.98
  58.7 0.6 fusion.97
  59.4 0.6 fusion.96
  60.0 6.0 %all-to-all-start.2 = ((f32[1,16,128,128]{3,1,0,2:T(8,128)}), f32[1,16,128,128]{3,1,0,2:T(8,128)S(1)}, u32[]{:S(2)}, u32[]{:S(2)}) async-start(f32[1,16,128,128]{3,1,0,2:T(8,128)} %copy.41), calls=%async_computation.2 | async-start | bytes 2097152 | tf_op jit(solution)/shard_map/all_to_all | solution.py:99
  66.0 0.1 add_multiply_fusion
  66.1 26.3 %all-to-all-done.2 = f32[1,16,128,128]{3,1,0,2:T(8,128)S(1)} async-done(((f32[1,16,128,128]{3,1,0,2:T(8,128)}), f32[1,16,128,128]{3,1,0,2:T(8,128)S(1)}, u32[]{:S(2)}, u32[]{:S(2)}) %all-to-all-start.2) | async-done | bytes 1048608 | tf_op jit(solution)/shard_map/all_to_all | solution.py:99
  92.4 1.0 copy-done.1
  93.4 18.3 %all-to-all-start = ((f32[16,1,16,8,128]{4,3,2,1,0:T(8,128)}), f32[16,1,16,8,128]{4,3,2,1,0:T(8,128)S(1)}, u32[]{:S(2)}, u32[]{:S(2)}) async-start(f32[16,1,16,8,128]{4,3,2,1,0:T(8,128)} %fusion.96), calls=%async_computation | async-start | bytes 2097152 | tf_op jit(solution)/shard_map/all_to_all | solution.py:17
  111.7 0.1 fusion.222
  111.9 0.1 fusion.219
  111.9 1.6 copy.70
  113.6 0.6 copy.36
  114.2 0.1 copy.42
  114.3 2.2 convolution_bitcast_fusion
  116.5 1.6 copy.43
  118.1 17.1 %all-to-all-done = f32[16,1,16,8,128]{4,3,2,1,0:T(8,128)S(1)} async-done(((f32[16,1,16,8,128]{4,3,2,1,0:T(8,128)}), f32[16,1,16,8,128]{4,3,2,1,0:T(8,128)S(1)}, u32[]{:S(2)}, u32[]{:S(2)}) %all-to-all-start) | async-done | bytes 1048608 | tf_op jit(solution)/shard_map/all_to_all | solution.py:17
  135.2 7.3 %all-to-all-start.3 = ((f32[1,256,8,128]{3,2,0,1:T(8,128)}), f32[1,256,8,128]{3,2,0,1:T(8,128)}, u32[]{:S(2)}, u32[]{:S(2)}) async-start(f32[1,256,8,128]{3,2,0,1:T(8,128)} %copy.43), calls=%async_computation.3 | async-start | bytes 2097152 | tf_op jit(solution)/shard_map/all_to_all | solution.py:104
  142.5 0.0 all-reduce.7.cloned.1.call-start
  142.5 2.1 fusion.30
  144.6 2.0 fusion.48
  146.6 3.0 fusion.8
  149.7 3.1 fusion.7
  152.9 2.3 convolution_bitcast_fusion.1
  155.2 0.1 broadcast_add_fusion
  155.2 1.7 fusion.221
  156.9 43.6 %all-reduce.5.cloned.1.call-done = f32[524288]{0:T(1024)} async-done(((f32[524288]{0:T(1024)}), f32[524288]{0:T(1024)}) %all-reduce.5.cloned.1.call-update) | async-done | bytes 2097168
  200.6 2.2 multiply_reduce_fusion.13
  202.7 3.7 %stack.141 = f32[6]{0:T(128)S(1)} concatenate(f32[1]{0:T(128)} %bitcast.5, f32[1]{0:T(128)} %bitcast.7, f32[1]{0:T(128)} %bitcast.9, f32[1]{0:T(128)} %bitcast.10, f32[1]{0:T(128)} %bitcast.11, f32[1]{0:T(128)} %bitcast.12), dimensions={0} | concatenate | bytes 48 | tf_op jit(solution)/shard_map/stack | solution.py:47
  206.5 5.9 %fusion.14 = (f32[1,16,128,128]{3,2,1,0:T(8,128)S(1)}, f32[1,16,128,128]{3,2,1,0:T(8,128)}, f32[128,16,128]{0,2,1:T(8,128)S(1)}) fusion(f32[1,16,128,128]{3,2,1,0:T(8,128)S(1)} %copy-done, f32[1,16,16,8,128]{4,3,2,1,0:T(8,128)} %bitcast.72, f32[1,16,128,128]{3,2,1,0:T(8,128)} %convolution_bitcast_fusion.1), kind=kOutput, calls=%fused_computation.27 | convolution fusion | flops 406093824 | bytes 6291456 | tf_op jit(solution)/shard_map/ik,szxk->szxi/dot_general | solution.py:89
  212.3 2.4 fusion.20
  214.8 3.8 %stack.179 = f32[6]{0:T(128)S(1)} concatenate(f32[1]{0:T(128)} %bitcast.75, f32[1]{0:T(128)} %bitcast.77, f32[1]{0:T(128)} %bitcast.79, f32[1]{0:T(128)} %bitcast.80, f32[1]{0:T(128)} %bitcast.81, f32[1]{0:T(128)} %bitcast.83), dimensions={0} | concatenate | bytes 48 | tf_op jit(solution)/shard_map/stack | solution.py:47
  218.6 46.0 %all-reduce.7.cloned.1.call-done = (f32[256,8,128]{2,0,1:T(8,128)}, f32[256,8,128]{2,0,1:T(8,128)}) async-done(((f32[256,8,128]{2,0,1:T(8,128)}, f32[256,8,128]{2,0,1:T(8,128)}), (f32[256,8,128]{2,0,1:T(8,128)}, f32[256,8,128]{2,0,1:T(8,128)})) %all-reduce.7.cloned.1.call-update) | async-done | bytes 2097168 | tf_op jit(solution)/shard_map/psum | solution.py:114
  264.7 2.8 fusion.139
  267.5 1.9 multiply_reduce_fusion.2
  269.4 3.8 %stack.165 = f32[6]{0:T(128)S(1)} concatenate(f32[1]{0:T(128)} %bitcast.45, f32[1]{0:T(128)} %bitcast.46, f32[1]{0:T(128)} %bitcast.47, f32[1]{0:T(128)} %bitcast.48, f32[1]{0:T(128)} %bitcast.49, f32[1]{0:T(128)} %bitcast.50), dimensions={0} | concatenate | bytes 48 | tf_op jit(solution)/shard_map/stack | solution.py:47
  273.2 3.8 %stack.172 = f32[6]{0:T(128)S(1)} concatenate(f32[1]{0:T(128)} %bitcast.53, f32[1]{0:T(128)} %bitcast.54, f32[1]{0:T(128)} %bitcast.55, f32[1]{0:T(128)} %bitcast.56, f32[1]{0:T(128)} %bitcast.57, f32[1]{0:T(128)} %bitcast.58), dimensions={0} | concatenate | bytes 48 | tf_op jit(solution)/shard_map/stack | solution.py:47
  277.1 0.7 multiply_add_fusion
  277.7 39.3 %psum.23 = f32[6]{0:T(128)} all-reduce(f32[6]{0:T(128)S(1)} %multiply_add_fusion), channel_id=1, replica_groups=mesh['band'=16,'spin'=2] {'band','spin'}, use_global_device_ids=true, to_apply=%region_28.29 | all-reduce | flops 6 | bytes 48 | tf_op jit(solution)/shard_map/psum | solution.py:132
  (23 shorter events, 0.1 us)
Async XLA Ops:
  16.1 44.0 %all-to-all-start.1 = ((f32[1,16,128,128]{3,1,0,2:T(8,128)}), f32[1,16,128,128]{3,1,0,2:T(8,128)}, u32[]{:S(2)}, u32[]{:S(2)}) async-start(f32[1,16,128,128]{3,1,0,2:T(8,128)} %copy.34), calls=%async_computation.1 | async-start | bytes 2097152 | tf_op jit(solution)/shard_map/all_to_all | solution.py:101
  23.5 5.2 %copy-start.7 = (s32[1,2]{1,0:T(1,128)S(1)}, s32[1,2]{1,0:T(1,128)}, u32[]{:S(2)}) copy-start(s32[1,2]{1,0:T(1,128)} %param.8) | copy-start | bytes 28
  23.5 177.0 %all-reduce.5.cloned.1.call-start = ((), (), s32[]{:S(2)}) async-start(), calls=%async_computation.4 | async-start | bytes 4194304
  45.8 1.3 copy-start
  47.1 18.9 %copy-start.4 = (s32[3,16384]{1,0:T(4,128)S(1)}, s32[3,16384]{1,0:T(4,128)}, u32[]{:S(2)}) copy-start(s32[3,16384]{1,0:T(4,128)} %param.9) | copy-start | bytes 589828
  47.1 18.9 %copy-start.5 = (f32[3]{0:T(128)S(1)}, f32[3]{0:T(128)}, u32[]{:S(2)}) copy-start(f32[3]{0:T(128)} %constant.139.clone) | copy-start | bytes 40
  60.0 32.4 %all-to-all-start.2 = ((f32[1,16,128,128]{3,1,0,2:T(8,128)}), f32[1,16,128,128]{3,1,0,2:T(8,128)S(1)}, u32[]{:S(2)}, u32[]{:S(2)}) async-start(f32[1,16,128,128]{3,1,0,2:T(8,128)} %copy.41), calls=%async_computation.2 | async-start | bytes 2097152 | tf_op jit(solution)/shard_map/all_to_all | solution.py:99
  92.4 1.0 copy-start.1
  93.4 41.9 %all-to-all-start = ((f32[16,1,16,8,128]{4,3,2,1,0:T(8,128)}), f32[16,1,16,8,128]{4,3,2,1,0:T(8,128)S(1)}, u32[]{:S(2)}, u32[]{:S(2)}) async-start(f32[16,1,16,8,128]{4,3,2,1,0:T(8,128)} %fusion.96), calls=%async_computation | async-start | bytes 2097152 | tf_op jit(solution)/shard_map/all_to_all | solution.py:17
  111.8 2.4 copy-start.2
  135.2 71.3 %all-to-all-start.3 = ((f32[1,256,8,128]{3,2,0,1:T(8,128)}), f32[1,256,8,128]{3,2,0,1:T(8,128)}, u32[]{:S(2)}, u32[]{:S(2)}) async-start(f32[1,256,8,128]{3,2,0,1:T(8,128)} %copy.43), calls=%async_computation.3 | async-start | bytes 2097152 | tf_op jit(solution)/shard_map/all_to_all | solution.py:104
  142.5 122.2 %all-reduce.7.cloned.1.call-start = ((), (), s32[]{:S(2)}) async-start(), calls=%async_computation.5 | async-start | bytes 4194304 | tf_op jit(solution)/shard_map/psum | solution.py:114
  206.5 5.9 %copy-start.3 = (f32[1,16,128,128]{3,2,1,0:T(8,128)S(1)}, f32[1,16,128,128]{3,2,1,0:T(8,128)}, u32[]{:S(2)}) copy-start(f32[1,16,128,128]{3,2,1,0:T(8,128)} %convolution_bitcast_fusion.1) | copy-start | bytes 3145732
  264.7 12.4 %copy-start.6 = (f32[6]{0:T(128)S(1)}, f32[6]{0:T(128)}, u32[]{:S(2)}) copy-start(f32[6]{0:T(128)} %constant.140.clone) | copy-start | bytes 76
Sparse Core Ops, SparseCore 0:
  45.9 154.6 all-reduce.4
  202.9 61.7 all-reduce.6
